TPU v7x, 32 devices: a whole 2x2x4 slice. The times are simulated.
32 devices in a mesh: tm: 4 (over y, x), sky: 8 (over z, core).
Axes of the slice: x: 2, y: 2, z: 4, core: 2. Of those that a mesh axis runs over, the one named last changes fastest.
Arguments:
- residual: float32 [16384, 128], P(('tm', 'sky')), may hold values from -110 to 110
- obs_weight: float32 [16384, 128], P(('tm', 'sky')), may hold values from 0.5 to 2
- source_partials: float32 [5, 16384, 128], P(None, ('tm', 'sky')), may hold values from -1 to 1
- attitude_partials: float32 [16, 16384, 128], P(None, ('tm', 'sky')), may hold values from -1.5 to 1.5
- source_index: int32 [16384, 128], P(('tm', 'sky')), may hold values from 0 to 127
- tile_pixel: int32 [16384], P(('tm', 'sky')), may hold values from 0 to 1023, as said below
- tile_knot: int32 [16384], P(('tm', 'sky')), may hold values from 0 to 2047, as said below
- pixel_slot: int32 [1024], replicated, may hold values from 0 to 1023, as said below
Outputs:
- final_residual: float32 [16384, 128], P(('tm', 'sky'))
- source_update: float32 [5, 131072], P(None, 'sky')
- attitude_update: float32 [4, 2048], P(None, 'tm')
Inputs may be any that keep to these rules, and one draw needn't show every extreme that they name: Tiles come in aligned blocks of 512; with owner = pixel_slot[tile_pixel[t]] // 128, no block holds more than 192 tiles of one owner, and every block holds exactly 192 tiles of some owner. `pixel_slot`: every slot number appears once. `tile_knot`: the tiles of aligned block q of 512 tiles have first knots in [q * 64, (q + 1) * 64).
All inputs are finite; a program needn't handle non-finite values.
Results may differ from a plain program's by a relative error of at most 0.0003.
Values sent between devices are 32-bit elements; how exact they have to be, the bound alone decides.
No kernel may reach another device: no remote copies, remote signals or barrier semaphores. Data moves between devices by JAX's collectives and lax.ppermute only.
A program may use at most 128 MiB of HBM per device.

v0:
```python
import math
import jax
import jax.numpy as jnp
from jax import lax
from jax.sharding import PartitionSpec as P

PIX_DEV = 128
SRC_PIX = 128
KNOTS_DEV = 512
SOURCE_PAIRS = tuple(((first, second) for first in range(5) for second in range(first, 5)))
KNOT_PAIRS = tuple(((first, second) for first in range(4) for second in range(first, 4)))


def passed_along(value, axis, steps):
    count = lax.axis_size(axis)
    first, last = (max(0, -steps), min(count, count - steps))
    return lax.ppermute(value, axis, [(source, source + steps) for source in range(first, last)])


def damped_solve(normal, target, order, pairs):
    entries = {}
    for number, couple in enumerate(pairs):
        entries[couple] = normal[number]
    factor = {}
    for column in range(order):
        pivot_value = entries[column, column] + 1.0
        for earlier in range(column):
            pivot_value = pivot_value - factor[column, earlier] * factor[column, earlier]
        pivot_value = jnp.sqrt(pivot_value)
        factor[column, column] = pivot_value
        for below in range(column + 1, order):
            current = entries[column, below]
            for earlier in range(column):
                current = current - factor[below, earlier] * factor[column, earlier]
            factor[below, column] = current / pivot_value
    forward = []
    for column in range(order):
        current = target[column]
        for earlier in range(column):
            current = current - factor[column, earlier] * forward[earlier]
        forward.append(current / factor[column, column])
    answer = [None] * order
    for column in reversed(range(order)):
        current = forward[column]
        for later in range(column + 1, order):
            current = current - factor[later, column] * answer[later]
        answer[column] = current / factor[column, column]
    return jnp.stack(answer)


def knot_terms(weights, partials, baseline):
    result = []
    for segment in range(4):
        portion = partials[4 * segment : 4 * segment + 4]
        sums_rows = [
            jnp.sum(weights * portion[first] * portion[second], axis=-1)
            for first, second in KNOT_PAIRS
        ]
        sums_rows = sums_rows + [
            jnp.sum(weights * portion[first] * baseline, axis=-1) for first in range(4)
        ]
        result.append(jnp.stack(sums_rows))
    return result


def correct(baseline, partials, picked):
    accumulated = partials[0] * picked[0]
    for component in range(1, partials.shape[0]):
        accumulated = accumulated + partials[component] * picked[component]
    return baseline - accumulated


def pixel_sums(products, indices, owners, capacity):

    def add_sender(sender, running):
        offset = sender * capacity
        portion = lax.dynamic_slice_in_dim(products, offset, capacity, 1)
        chosen = lax.dynamic_slice_in_dim(indices, offset, capacity, 0)
        within = ((chosen % SRC_PIX)[:, :, None] == jnp.arange(SRC_PIX, dtype=jnp.int32)).astype(
            jnp.float32
        )
        pixel_hits = (
            (chosen[:, 0] // SRC_PIX)[:, None] == jnp.arange(PIX_DEV, dtype=jnp.int32)
        ).astype(jnp.float32)
        spread = jnp.einsum("ctk,tks->cts", portion, within, precision=lax.Precision.HIGHEST)
        return running + jnp.einsum(
            "cts,tp->cps", spread, pixel_hits, precision=lax.Precision.HIGHEST
        )

    running = lax.fori_loop(0, owners, add_sender, jnp.zeros((20, PIX_DEV, SRC_PIX), jnp.float32))
    return running.reshape(20, PIX_DEV * SRC_PIX)


def pick_sources(update, indices, rows):
    pixels = update.shape[1] // SRC_PIX
    table = update.reshape(update.shape[0], pixels, SRC_PIX)
    blocks = indices.shape[0] // rows

    def fill(number, output):
        offset = number * rows
        chosen = lax.dynamic_slice_in_dim(indices, offset, rows, 0)
        pixel_hits = (
            (chosen[:, 0] // SRC_PIX)[:, None] == jnp.arange(pixels, dtype=jnp.int32)
        ).astype(jnp.float32)
        within = ((chosen % SRC_PIX)[:, :, None] == jnp.arange(SRC_PIX, dtype=jnp.int32)).astype(
            jnp.float32
        )
        row_values = jnp.einsum("tp,cps->cts", pixel_hits, table, precision=lax.Precision.HIGHEST)
        picked = jnp.einsum("cts,tks->ctk", row_values, within, precision=lax.Precision.HIGHEST)
        return lax.dynamic_update_slice_in_dim(output, picked, offset, 1)

    empty = jnp.zeros((update.shape[0], indices.shape[0], indices.shape[1]), jnp.float32)
    return lax.fori_loop(0, blocks, fill, empty)


def body(
    residual,
    obs_weight,
    source_partials,
    attitude_partials,
    source_index,
    tile_pixel,
    tile_knot,
    pixel_slot,
):
    owners = lax.axis_size("sky")
    tiles = residual.shape[0]
    capacity = 3 * tiles // owners
    pixels = pixel_slot.shape[0]
    pixel_match = (tile_pixel[:, None] == jnp.arange(pixels, dtype=jnp.int32)[None, :]).astype(
        jnp.float32
    )
    seats_float = jnp.dot(
        pixel_match, pixel_slot.astype(jnp.float32), precision=lax.Precision.HIGHEST
    )
    seats = seats_float.astype(jnp.int32)
    owner_ids = seats // PIX_DEV
    local_pixel = seats % PIX_DEV
    member = (owner_ids[:, None] == jnp.arange(owners, dtype=jnp.int32)[None, :]).astype(
        jnp.float32
    )
    tile_numbers = jnp.arange(tiles, dtype=jnp.int32)
    lower = (tile_numbers[:, None] > tile_numbers[None, :]).astype(jnp.float32)
    before = jnp.dot(lower, member, precision=lax.Precision.HIGHEST)
    position = jnp.sum(before * member, axis=1).astype(jnp.int32)
    slot_index = owner_ids * capacity + position
    place = (jnp.arange(owners * capacity, dtype=jnp.int32)[:, None] == slot_index[None, :]).astype(
        jnp.float32
    )
    local_source = (local_pixel[:, None] * SRC_PIX + source_index).astype(jnp.float32)
    sent_index = jnp.dot(place, local_source, precision=lax.Precision.HIGHEST).astype(jnp.int32)[
        None
    ]
    root_weight = jnp.sqrt(obs_weight)
    fields = jnp.concatenate(
        [(root_weight * residual)[None], root_weight[None] * source_partials], axis=0
    )
    packed = jnp.einsum("st,ctk->csk", place, fields, precision=lax.Precision.HIGHEST)
    arrived, arrived_index = (
        lax.all_to_all(packed, "sky", split_axis=1, concat_axis=1, tiled=True),
        lax.all_to_all(sent_index, "sky", split_axis=1, concat_axis=1, tiled=True),
    )
    scaled = arrived[1:]
    products = [scaled[first] * scaled[second] for first, second in SOURCE_PAIRS]
    products = jnp.stack(products + [scaled[first] * arrived[0] for first in range(5)])
    normals = pixel_sums(products, arrived_index[0], owners, capacity)
    summed = lax.psum(normals, "tm")
    source_update = damped_solve(summed[:15], summed[15:], 5, SOURCE_PAIRS)
    everything = lax.all_gather(source_update, "sky", axis=1, tiled=True)
    global_source = seats[:, None] * SRC_PIX + source_index
    picked = pick_sources(everything, global_source, math.gcd(tiles, 64))
    settled = correct(residual, source_partials, picked)
    knot_start = tile_knot - lax.axis_index("tm") * KNOTS_DEV
    knot_hits = (knot_start[:, None] == jnp.arange(KNOTS_DEV, dtype=jnp.int32)[None, :]).astype(
        jnp.float32
    )
    accumulated = jnp.zeros((14, KNOTS_DEV + 3), jnp.float32)
    for segment, tile_sums in enumerate(knot_terms(obs_weight, attitude_partials, settled)):
        placed = jnp.dot(tile_sums, knot_hits, precision=lax.Precision.HIGHEST)
        accumulated = accumulated + jnp.pad(placed, ((0, 0), (segment, 3 - segment)))
    arriving = passed_along(accumulated[:, KNOTS_DEV:], "tm", 1)
    own_rows = accumulated[:, :KNOTS_DEV] + jnp.pad(arriving, ((0, 0), (0, KNOTS_DEV - 3)))
    whole = lax.psum(own_rows, "sky")
    attitude_update = damped_solve(whole[:10], whole[10:], 4, KNOT_PAIRS)
    following = passed_along(attitude_update[:, :3], "tm", -1)
    extended = jnp.concatenate([attitude_update, following], axis=1)
    accumulated_fix = None
    for segment in range(4):
        window = extended[:, segment : segment + KNOTS_DEV]
        values = jnp.dot(window, knot_hits.T, precision=lax.Precision.HIGHEST)
        for component in range(4):
            addend = attitude_partials[4 * segment + component] * values[component][:, None]
            accumulated_fix = addend if accumulated_fix is None else accumulated_fix + addend
    final_residual = settled - accumulated_fix
    return (final_residual, source_update, attitude_update)


def solution(mesh):
    in_specs = (
        P(("tm", "sky"), None),
        P(("tm", "sky"), None),
        P(None, ("tm", "sky"), None),
        P(None, ("tm", "sky"), None),
        P(("tm", "sky"), None),
        P(("tm", "sky")),
        P(("tm", "sky")),
        P(),
    )
    out_specs = (P(("tm", "sky"), None), P(None, "sky"), P(None, "tm"))
    return jax.shard_map(body, mesh=mesh, in_specs=in_specs, out_specs=out_specs, check_vma=False)
```

profile of v0, /device:TPU:0, one launch (start us, length us, event | category | flops | bytes accessed | tf_op | source)
XLA Modules:
  0.0 626.5 jit_solution(8565217620249601764)
XLA Ops:
  12.9 6.0 convolution_bitcast_fusion.1
  18.8 6.2 copy.44
  25.0 6.5 %all-to-all-start.1 = ((f32[6,1536,128]{2,0,1:T(8,128)}), f32[6,1536,128]{2,0,1:T(8,128)}, u32[]{:S(2)}, u32[]{:S(2)}) async-start(f32[6,1536,128]{2,0,1:T(8,128)} %copy.44), calls=%async_computation.1 | async-start | bytes 12582912 | tf_op jit(solution)/shard_map/all_to_all | solution.py:160
  34.0 136.5 %all-to-all-done.1 = f32[6,1536,128]{2,0,1:T(8,128)} async-done(((f32[6,1536,128]{2,0,1:T(8,128)}), f32[6,1536,128]{2,0,1:T(8,128)}, u32[]{:S(2)}, u32[]{:S(2)}) %all-to-all-start.1) | async-done | bytes 4718624 | tf_op jit(solution)/shard_map/all_to_all | solution.py:160
  170.5 4.2 all-to-all-start
  175.0 22.1 %slice_multiply_fusion = (f32[1,1536,128]{2,0,1:T(1,128)S(1)}, f32[1,1536,128]{2,0,1:T(1,128)S(1)}, f32[1,1536,128]{2,0,1:T(1,128)}, f32[1,1536,128]{2,0,1:T(1,1...) fusion(f32[6,1536,128]{2,0,1:T(8,128)} %all-to-all-done.1), kind=kLoop, calls=%fused_computation.340 | loop fusion | flops 2359296 | bytes 14155776 | tf_op jit(solution)/shard_map/mul | solution.py:165
  197.1 20.9 %slice_multiply_fusion.1 = (f32[1,1536,128]{2,0,1:T(1,128)}, f32[1,1536,128]{2,0,1:T(1,128)}, f32[1,1536,128]{2,0,1:T(1,128)}, f32[1,1536,128]{2,0,1:T(1,128)}, ...) fusion(f32[6,1536,128]{2,0,1:T(8,128)} %all-to-all-done.1), kind=kLoop, calls=%fused_computation.341 | loop fusion | flops 1572864 | bytes 11010048 | tf_op jit(solution)/shard_map/mul | solution.py:165
  218.0 49.6 %stack.218 = f32[20,1536,128]{2,0,1:T(8,128)} concatenate(f32[1,1536,128]{2,0,1:T(1,128)} %get-tuple-element.400, f32[1,1536,128]{2,0,1:T(1,128)} %get-tuple-element.408, f32[1,1536,128]{2,0,1:T(1,128)} %get-tuple-element.407, f32[1,1536,128]{2,0,1:T(1,128)} %get-tuple-element.406, f32[1,1536,128]{2,0,1:T(1,128)} %get-tuple-element.405, f32[1,1536,128]{2,0,1:T(1,128)S(1)} %get-tuple-element.390, ...), dimensions={0} | concatenate | bytes 31457280 | tf_op jit(solution)/shard_map/stack | solution.py:165
  267.7 114.9 %while.32 = (s32[]{:T(128)}, f32[20,128,128]{2,1,0:T(8,128)S(1)}, s32[1536,128]{1,0:T(8,128)}, f32[20,1536,128]{2,0,1:T(8,128)}, s32[]{:T(128)}, /*index=5*/s32[]{:T(128)}, s32[]{:T(128)}, s32[]{:T(128)}) while((s32[]{:T(128)}, f32[20,128,128]{2,1,0:T(8,128)S(1)}, s32[1536,128]{1,0:T(8,128)}, f32[20,1536,128]{2,0,1:T(8,128)}, ...), condition=%wide.region_2.3_spmd.clone, body=%wide.region_1.2_spmd.clone.sunk | while | flops 1514048256 | bytes 9800085 | solution.py:90
  268.8 9.9 %fusion.206 = f32[20,192,128]{2,0,1:T(8,128)} fusion(f32[20,1536,128]{2,0,1:T(8,128)} %get-tuple-element.501, s32[]{:T(128)S(6)} %select_n.124, s32[192,128]{1,0:T(8,128)S(1)} %copy.140), kind=kOutput, calls=%fused_computation.26.clone.1 | convolution fusion | flops 758120448 | bytes 4423684 | tf_op jit(solution)/shard_map/while/body/eval_jaxpr/ctk,tks->cts/dot_general | solution.py:85
  283.2 9.9 %fusion.206 = f32[20,192,128]{2,0,1:T(8,128)} fusion(f32[20,1536,128]{2,0,1:T(8,128)} %get-tuple-element.501, s32[]{:T(128)S(6)} %select_n.124, s32[192,128]{1,0:T(8,128)S(1)} %copy.140), kind=kOutput, calls=%fused_computation.26.clone.1 | convolution fusion | flops 758120448 | bytes 4423684 | tf_op jit(solution)/shard_map/while/body/eval_jaxpr/ctk,tks->cts/dot_general | solution.py:85
  297.6 9.9 %fusion.206 = f32[20,192,128]{2,0,1:T(8,128)} fusion(f32[20,1536,128]{2,0,1:T(8,128)} %get-tuple-element.501, s32[]{:T(128)S(6)} %select_n.124, s32[192,128]{1,0:T(8,128)S(1)} %copy.140), kind=kOutput, calls=%fused_computation.26.clone.1 | convolution fusion | flops 758120448 | bytes 4423684 | tf_op jit(solution)/shard_map/while/body/eval_jaxpr/ctk,tks->cts/dot_general | solution.py:85
  311.9 9.9 %fusion.206 = f32[20,192,128]{2,0,1:T(8,128)} fusion(f32[20,1536,128]{2,0,1:T(8,128)} %get-tuple-element.501, s32[]{:T(128)S(6)} %select_n.124, s32[192,128]{1,0:T(8,128)S(1)} %copy.140), kind=kOutput, calls=%fused_computation.26.clone.1 | convolution fusion | flops 758120448 | bytes 4423684 | tf_op jit(solution)/shard_map/while/body/eval_jaxpr/ctk,tks->cts/dot_general | solution.py:85
  326.3 9.9 %fusion.206 = f32[20,192,128]{2,0,1:T(8,128)} fusion(f32[20,1536,128]{2,0,1:T(8,128)} %get-tuple-element.501, s32[]{:T(128)S(6)} %select_n.124, s32[192,128]{1,0:T(8,128)S(1)} %copy.140), kind=kOutput, calls=%fused_computation.26.clone.1 | convolution fusion | flops 758120448 | bytes 4423684 | tf_op jit(solution)/shard_map/while/body/eval_jaxpr/ctk,tks->cts/dot_general | solution.py:85
  340.6 9.9 %fusion.206 = f32[20,192,128]{2,0,1:T(8,128)} fusion(f32[20,1536,128]{2,0,1:T(8,128)} %get-tuple-element.501, s32[]{:T(128)S(6)} %select_n.124, s32[192,128]{1,0:T(8,128)S(1)} %copy.140), kind=kOutput, calls=%fused_computation.26.clone.1 | convolution fusion | flops 758120448 | bytes 4423684 | tf_op jit(solution)/shard_map/while/body/eval_jaxpr/ctk,tks->cts/dot_general | solution.py:85
  355.0 9.9 %fusion.206 = f32[20,192,128]{2,0,1:T(8,128)} fusion(f32[20,1536,128]{2,0,1:T(8,128)} %get-tuple-element.501, s32[]{:T(128)S(6)} %select_n.124, s32[192,128]{1,0:T(8,128)S(1)} %copy.140), kind=kOutput, calls=%fused_computation.26.clone.1 | convolution fusion | flops 758120448 | bytes 4423684 | tf_op jit(solution)/shard_map/while/body/eval_jaxpr/ctk,tks->cts/dot_general | solution.py:85
  369.4 9.9 %fusion.206 = f32[20,192,128]{2,0,1:T(8,128)} fusion(f32[20,1536,128]{2,0,1:T(8,128)} %get-tuple-element.501, s32[]{:T(128)S(6)} %select_n.124, s32[192,128]{1,0:T(8,128)S(1)} %copy.140), kind=kOutput, calls=%fused_computation.26.clone.1 | convolution fusion | flops 758120448 | bytes 4423684 | tf_op jit(solution)/shard_map/while/body/eval_jaxpr/ctk,tks->cts/dot_general | solution.py:85
  385.1 61.7 %all-reduce.7.cloned.1.call-done = f32[20,16384]{1,0:T(8,128)} async-done(((f32[20,16384]{1,0:T(8,128)}), f32[20,16384]{1,0:T(8,128)}) %all-reduce.7.cloned.1.call-update) | async-done | bytes 1310736 | tf_op jit(solution)/shard_map/psum | solution.py:167
  446.8 5.2 fusion.141
  468.1 40.0 %all-gather.2.cloned.1.call-done = f32[5,131072]{1,0:T(8,128)} async-done(((f32[5,16384]{1,0:T(8,128)}), f32[5,131072]{1,0:T(8,128)}) %all-gather.2.cloned.1.call-update) | async-done | bytes 2621456 | tf_op jit(solution)/shard_map/all_gather | solution.py:169
  511.9 55.2 %while.31 = (s32[]{:T(128)}, f32[5,512,128]{2,1,0:T(8,128)}, s32[512,128]{0,1:T(8,128)S(1)}, f32[5,1024,128]{2,1,0:T(8,128)S(1)}, s32[]{:T(128)}, /*index=5*/s32[]{:T(128)}, s32[]{:T(128)}, s32[]{:T(128)}) while((s32[]{:T(128)}, f32[5,512,128]{2,1,0:T(8,128)}, s32[512,128]{0,1:T(8,128)S(1)}, f32[5,1024,128]{2,1,0:T(8,128)S(1)}, s32[]{:T(128)}, ...), condition=%wide.region_5.6_spmd, body=%wide.region_4.5_spmd.sunk | while | flops 567436224 | bytes 3605391 | solution.py:113
  513.4 4.8 fusion.202
  520.2 4.8 fusion.202
  527.1 4.8 fusion.202
  534.1 4.8 fusion.202
  541.0 4.8 fusion.202
  547.8 4.8 fusion.202
  554.8 4.8 fusion.202
  561.7 4.8 fusion.202
  580.5 25.9 %psum.15 = f32[14,512]{1,0:T(8,128)S(1)} all-reduce(f32[14,512]{1,0:T(8,128)S(1)} %slice_add_fusion.5), channel_id=1, replica_groups=mesh['tm'=4,'sky'=8] {'sky'}, use_global_device_ids=true, to_apply=%region_62.63 | all-reduce | flops 7168 | bytes 57344 | tf_op jit(solution)/shard_map/psum | solution.py:183
  608.6 4.4 collective-permute-done.1
  615.0 4.6 fusion.61
  (169 shorter events, 100.1 us)
Async XLA Ops:
  7.2 5.1 copy-start.1
  25.0 6.5 %copy-start.8 = (s32[512,128]{1,0:T(8,128)S(1)}, s32[512,128]{1,0:T(8,128)}, u32[]{:S(2)}) copy-start(s32[512,128]{1,0:T(8,128)} %param.16) | copy-start | bytes 786436
  25.0 145.5 %all-to-all-start.1 = ((f32[6,1536,128]{2,0,1:T(8,128)}), f32[6,1536,128]{2,0,1:T(8,128)}, u32[]{:S(2)}, u32[]{:S(2)}) async-start(f32[6,1536,128]{2,0,1:T(8,128)} %copy.44), calls=%async_computation.1 | async-start | bytes 12582912 | tf_op jit(solution)/shard_map/all_to_all | solution.py:160
  170.5 97.1 %all-to-all-start = ((s32[1,1536,128]{2,0,1:T(1,128)}), s32[1,1536,128]{2,0,1:T(1,128)}, u32[]{:S(2)}, u32[]{:S(2)}) async-start(s32[1,1536,128]{2,0,1:T(1,128)} %bitcast.7), calls=%async_computation | async-start | bytes 1572864 | tf_op jit(solution)/shard_map/all_to_all | solution.py:161
  174.7 272.1 %all-reduce.7.cloned.1.call-start = ((), (), s32[]{:S(2)}) async-start(), calls=%async_computation.2 | async-start | bytes 3145728 | tf_op jit(solution)/shard_map/psum | solution.py:167
  384.8 123.3 %all-gather.2.cloned.1.call-start = ((), (), s32[]{:S(2)}) async-start(), calls=%async_computation.3 | async-start | bytes 4718592 | tf_op jit(solution)/shard_map/all_gather | solution.py:169
  456.0 5.2 copy-start.10
  456.0 5.3 copy-start.2
  567.1 3.7 copy-start
  567.1 3.7 copy-start.3
  567.1 3.8 copy-start.4
  567.1 3.9 copy-start.5
  567.1 3.9 copy-start.6
  567.1 4.0 copy-start.7
  575.8 4.7 collective-permute-start
  606.6 13.0 %copy-start.9 = (f32[4,512]{1,0:T(4,128)}, f32[4,512]{1,0:T(4,128)S(1)}, u32[]{:S(2)}) copy-start(f32[4,512]{1,0:T(4,128)S(1)} %pad_maximum_fusion.1) | copy-start | bytes 24580
  607.3 5.7 collective-permute-start.1
Sparse Core Ops, SparseCore 0:
  384.9 61.8 all-reduce.6
  461.2 46.8 all-gather.1
where the time goes:
time: 634 us; the launch traced here: 626 us
  waiting for transfers between devices  244 us (38%)
  matrix products  168 us (26%)
  local copies, waits for them, and re-layouts  81.4 us (13%)
  other arithmetic  76.7 us (12%)
  blocking collectives  25.9 us (4%)
  starting transfers between devices  15.8 us (2%)
  between operations  14.4 us (2%)
    all_to_all x1, waiting for transfers between devices, body(): lax.all_to_all(packed, 'sky', split_axis=1, concat_axis=1, tiled=True)  137 us
    dot_general x8, matrix products, add_sender(): jnp.einsum('ctk,tks->cts', portion, within, precision=lax.Precision.HIGHEST)  79.5 us
    psum x1, waiting for transfers between devices, body(): summed = lax.psum(normals, 'tm')  61.7 us
    another operation x1, local copies, waits for them, and re-layouts, body(): jnp.stack(products + [scaled[first] * arrived[0] for first in range(5)])  49.6 us
    mul x2, other arithmetic, body(): scaled[first] * arrived[0]  43.1 us
    all_gather x1, waiting for transfers between devices, body(): everything = lax.all_gather(source_update, 'sky', axis=1, tiled=True)  40 us
    dot_general x8, matrix products, fill(): jnp.einsum('cts,tks->ctk', row_values, within, precision=lax.Precision.HI...  38 us
    psum x1, blocking collectives, body(): whole = lax.psum(own_rows, 'sky')  25.9 us
  transfers between devices with their start and end apart: 6, of which 5 were waited for; matrix products, arithmetic and copies ran while one was open for 16% of the time, Pallas kernels for 0%

commit v1 on v0

--- a/solution.py
+++ b/solution.py
@@ -9,6 +9,28 @@
 KNOTS_DEV = 512
 SOURCE_PAIRS = tuple(((first, second) for first in range(5) for second in range(first, 5)))
 KNOT_PAIRS = tuple(((first, second) for first in range(4) for second in range(first, 4)))
+
+
+def cut_along(shard, dim, size):
+    before, after = (shard.shape[:dim], shard.shape[dim + 1 :])
+    return jnp.moveaxis(shard.reshape(*before, size, -1, *after), dim, 0)
+
+
+def joined_along(blocks, dim):
+    dims = list(blocks.shape[1:])
+    dims[dim] *= blocks.shape[0]
+    return jnp.moveaxis(blocks, 0, dim).reshape(dims)
+
+
+def pairwise_exchange(x, axis, split_dim, concat_dim):
+    devices, index = (lax.axis_size(axis), lax.axis_index(axis))
+    tiles = cut_along(x, split_dim, devices)
+    outs = [tiles[index]]
+    for step in range(1, devices):
+        sent = tiles[index ^ step]
+        outs.append(lax.ppermute(sent, axis, [(i, i ^ step) for i in range(devices)]))
+    tiles = jnp.stack(outs)[index ^ jnp.arange(devices)]
+    return joined_along(tiles, concat_dim)
 
 
 def passed_along(value, axis, steps):
@@ -157,7 +179,7 @@
     )
     packed = jnp.einsum("st,ctk->csk", place, fields, precision=lax.Precision.HIGHEST)
     arrived, arrived_index = (
-        lax.all_to_all(packed, "sky", split_axis=1, concat_axis=1, tiled=True),
+        pairwise_exchange(packed, "sky", 1, 1),
         lax.all_to_all(sent_index, "sky", split_axis=1, concat_axis=1, tiled=True),
     )
     scaled = arrived[1:]

time: 634 us -> 586 us (0.924)
  waiting for transfers between devices: 244 us -> 201 us
  other arithmetic: 76.7 us -> 42 us
  local copies, waits for them, and re-layouts: 81.4 us -> 105 us
    all_to_all x1 -> x0, waiting for transfers between devices: 137 us -> none  [body(): lax.all_to_all(packed, 'sky', split_axis=1, concat_axis=1, tiled=True)]
    ppermute x0 -> x7, waiting for transfers between devices: none -> 64.7 us  [pairwise_exchange(): lax.ppermute(sent, axis, [(i, i ^ step) for i in range(devices)])]
    mul x2, other arithmetic: 43.1 us -> 8.47 us  [body(): scaled[first] * arrived[0]]
    psum x1, waiting for transfers between devices: 61.7 us -> 91 us  [body(): summed = lax.psum(normals, 'tm')]
    unnamed x29 -> x38, local copies, waits for them, and re-layouts: 8.03 us -> 21.8 us
    ppermute x0 -> x7, starting transfers between devices: none -> 10.1 us  [pairwise_exchange(): lax.ppermute(sent, axis, [(i, i ^ step) for i in range(devices)])]
    all_to_all x1 -> x0, starting transfers between devices: 6.49 us -> none  [body(): lax.all_to_all(packed, 'sky', split_axis=1, concat_axis=1, tiled=True)]
  transfers between devices with their start and end apart: 6 -> 12, of which waited for: 5 -> 8; matrix products, arithmetic and copies ran while one was open for 16% -> 15% of each run, Pallas kernels for 0% -> 0%
where the time goes in v1:
time: 586 us; the launch traced here: 577 us
  waiting for transfers between devices  201 us (34%)
  matrix products  168 us (29%)
  local copies, waits for them, and re-layouts  105 us (18%)
  other arithmetic  42 us (7%)
  blocking collectives  25.9 us (4%)
  starting transfers between devices  20 us (3%)
  between operations  14.4 us (2%)
    psum x1, waiting for transfers between devices, body(): summed = lax.psum(normals, 'tm')  91 us
    dot_general x8, matrix products, add_sender(): jnp.einsum('ctk,tks->cts', portion, within, precision=lax.Precision.HIGHEST)  79.5 us
    ppermute x7, waiting for transfers between devices, pairwise_exchange(): lax.ppermute(sent, axis, [(i, i ^ step) for i in range(devices)])  64.7 us
    another operation x1, local copies, waits for them, and re-layouts, body(): jnp.stack(products + [scaled[first] * arrived[0] for first in range(5)])  49.6 us
    all_gather x1, waiting for transfers between devices, body(): everything = lax.all_gather(source_update, 'sky', axis=1, tiled=True)  40 us
    dot_general x8, matrix products, fill(): jnp.einsum('cts,tks->ctk', row_values, within, precision=lax.Precision.HI...  38 us
    psum x1, blocking collectives, body(): whole = lax.psum(own_rows, 'sky')  25.9 us
    dot_general x8, matrix products, add_sender(): jnp.einsum('cts,tp->cps', spread, pixel_hits, precision=lax.Precision.HIG...  25.8 us
  transfers between devices with their start and end apart: 12, of which 8 were waited for; matrix products, arithmetic and copies ran while one was open for 15% of the time, Pallas kernels for 0%

profile of v1, /device:TPU:0, one launch (start us, length us, event | category | flops | bytes accessed | tf_op | source)
XLA Modules:
  0.0 577.3 jit_solution(4861496219282790001)
XLA Ops:
  14.1 6.1 %convolution_bitcast_fusion.1 = f32[6,1536,128]{1,2,0:T(8,128)} fusion(f32[5,512,128]{1,2,0:T(8,128)S(1)} %broadcast_multiply_fusion, f32[1,512,128]{1,2,0:T(8,128)S(1)} %get-tuple-element.414, s32[512]{0:T(512)S(1)} %convert_add_fusion), kind=kOutput, calls=%fused_computation.43 | convolution fusion | flops 7248936960 | bytes 6293504 | tf_op jit(solution)/shard_map/st,ctk->csk/dot_general | solution.py:180
  20.2 6.0 %copy.43 = f32[6,1536,128]{2,1,0:T(8,128)} copy(f32[6,1536,128]{1,2,0:T(8,128)} %convolution_bitcast_fusion.1) | data formatting | bytes 9437184 | tf_op jit(solution)/shard_map/st,ctk->csk/transpose | solution.py:180
  38.4 4.9 all-to-all-start
  51.1 21.3 %collective-permute-done.1 = f32[6,192,128]{2,1,0:T(8,128)} collective-permute-done((f32[6,192,128]{2,1,0:T(8,128)}, f32[6,192,128]{2,1,0:T(8,128)}, u32[]{:S(2)}, u32[]{:S(2)}) %collective-permute-start.1) | collective-permute-done | bytes 589856 | tf_op jit(solution)/shard_map/ppermute | solution.py:31
  74.8 9.8 %collective-permute-done.2 = f32[6,192,128]{2,1,0:T(8,128)} collective-permute-done((f32[6,192,128]{2,1,0:T(8,128)}, f32[6,192,128]{2,1,0:T(8,128)}, u32[]{:S(2)}, u32[]{:S(2)}) %collective-permute-start.2) | collective-permute-done | bytes 589856 | tf_op jit(solution)/shard_map/ppermute | solution.py:31
  90.4 22.8 %collective-permute-done.5 = f32[6,192,128]{2,1,0:T(8,128)S(1)} collective-permute-done((f32[6,192,128]{2,1,0:T(8,128)S(1)}, f32[6,192,128]{2,1,0:T(8,128)S(1)}, u32[]{:S(2)}, u32[]{:S(2)}) %collective-permute-start.5) | collective-permute-done | bytes 589856 | tf_op jit(solution)/shard_map/ppermute | solution.py:31
  114.1 10.8 %collective-permute-done.6 = f32[6,192,128]{2,1,0:T(8,128)S(1)} collective-permute-done((f32[6,192,128]{2,1,0:T(8,128)S(1)}, f32[6,192,128]{2,1,0:T(8,128)S(1)}, u32[]{:S(2)}, u32[]{:S(2)}) %collective-permute-start.6) | collective-permute-done | bytes 589856 | tf_op jit(solution)/shard_map/ppermute | solution.py:31
  125.8 5.3 gather_fusion
  131.2 5.3 slice_multiply_fusion.1
  139.6 49.6 %stack.250 = f32[20,1536,128]{2,0,1:T(8,128)} concatenate(f32[1,1536,128]{2,0,1:T(1,128)} %bitcast.530, f32[1,1536,128]{2,0,1:T(1,128)} %bitcast.538, f32[1,1536,128]{2,0,1:T(1,128)} %bitcast.537, f32[1,1536,128]{2,0,1:T(1,128)} %bitcast.536, f32[1,1536,128]{2,0,1:T(1,128)} %bitcast.535, f32[1,1536,128]{2,0,1:T(1,128)S(1)} %bitcast.520, f32[1,1536,128]{2,0,1:T(1,128)} %bitcast.521, ...), dimensions={0} | concatenate | bytes 31457280 | tf_op jit(solution)/shard_map/stack | solution.py:187
  189.3 114.9 %while.32 = (s32[]{:T(128)}, f32[20,128,128]{2,1,0:T(8,128)S(1)}, s32[1536,128]{1,0:T(8,128)}, f32[20,1536,128]{2,0,1:T(8,128)}, s32[]{:T(128)}, /*index=5*/s32[]{:T(128)}, s32[]{:T(128)}, s32[]{:T(128)}) while((s32[]{:T(128)}, f32[20,128,128]{2,1,0:T(8,128)S(1)}, s32[1536,128]{1,0:T(8,128)}, f32[20,1536,128]{2,0,1:T(8,128)}, ...), condition=%wide.region_2.3_spmd.clone, body=%wide.region_1.2_spmd.clone.sunk | while | flops 1514048256 | bytes 9800085 | solution.py:112
  190.4 9.9 %fusion.207 = f32[20,192,128]{2,0,1:T(8,128)} fusion(f32[20,1536,128]{2,0,1:T(8,128)} %get-tuple-element.504, s32[]{:T(128)S(6)} %select_n.170, s32[192,128]{1,0:T(8,128)S(1)} %copy.159), kind=kOutput, calls=%fused_computation.27.clone.1 | convolution fusion | flops 758120448 | bytes 4423684 | tf_op jit(solution)/shard_map/while/body/eval_jaxpr/ctk,tks->cts/dot_general | solution.py:107
  204.8 9.9 %fusion.207 = f32[20,192,128]{2,0,1:T(8,128)} fusion(f32[20,1536,128]{2,0,1:T(8,128)} %get-tuple-element.504, s32[]{:T(128)S(6)} %select_n.170, s32[192,128]{1,0:T(8,128)S(1)} %copy.159), kind=kOutput, calls=%fused_computation.27.clone.1 | convolution fusion | flops 758120448 | bytes 4423684 | tf_op jit(solution)/shard_map/while/body/eval_jaxpr/ctk,tks->cts/dot_general | solution.py:107
  219.1 9.9 %fusion.207 = f32[20,192,128]{2,0,1:T(8,128)} fusion(f32[20,1536,128]{2,0,1:T(8,128)} %get-tuple-element.504, s32[]{:T(128)S(6)} %select_n.170, s32[192,128]{1,0:T(8,128)S(1)} %copy.159), kind=kOutput, calls=%fused_computation.27.clone.1 | convolution fusion | flops 758120448 | bytes 4423684 | tf_op jit(solution)/shard_map/while/body/eval_jaxpr/ctk,tks->cts/dot_general | solution.py:107
  233.5 9.9 %fusion.207 = f32[20,192,128]{2,0,1:T(8,128)} fusion(f32[20,1536,128]{2,0,1:T(8,128)} %get-tuple-element.504, s32[]{:T(128)S(6)} %select_n.170, s32[192,128]{1,0:T(8,128)S(1)} %copy.159), kind=kOutput, calls=%fused_computation.27.clone.1 | convolution fusion | flops 758120448 | bytes 4423684 | tf_op jit(solution)/shard_map/while/body/eval_jaxpr/ctk,tks->cts/dot_general | solution.py:107
  247.9 9.9 %fusion.207 = f32[20,192,128]{2,0,1:T(8,128)} fusion(f32[20,1536,128]{2,0,1:T(8,128)} %get-tuple-element.504, s32[]{:T(128)S(6)} %select_n.170, s32[192,128]{1,0:T(8,128)S(1)} %copy.159), kind=kOutput, calls=%fused_computation.27.clone.1 | convolution fusion | flops 758120448 | bytes 4423684 | tf_op jit(solution)/shard_map/while/body/eval_jaxpr/ctk,tks->cts/dot_general | solution.py:107
  262.2 9.9 %fusion.207 = f32[20,192,128]{2,0,1:T(8,128)} fusion(f32[20,1536,128]{2,0,1:T(8,128)} %get-tuple-element.504, s32[]{:T(128)S(6)} %select_n.170, s32[192,128]{1,0:T(8,128)S(1)} %copy.159), kind=kOutput, calls=%fused_computation.27.clone.1 | convolution fusion | flops 758120448 | bytes 4423684 | tf_op jit(solution)/shard_map/while/body/eval_jaxpr/ctk,tks->cts/dot_general | solution.py:107
  276.6 9.9 %fusion.207 = f32[20,192,128]{2,0,1:T(8,128)} fusion(f32[20,1536,128]{2,0,1:T(8,128)} %get-tuple-element.504, s32[]{:T(128)S(6)} %select_n.170, s32[192,128]{1,0:T(8,128)S(1)} %copy.159), kind=kOutput, calls=%fused_computation.27.clone.1 | convolution fusion | flops 758120448 | bytes 4423684 | tf_op jit(solution)/shard_map/while/body/eval_jaxpr/ctk,tks->cts/dot_general | solution.py:107
  291.0 9.9 %fusion.207 = f32[20,192,128]{2,0,1:T(8,128)} fusion(f32[20,1536,128]{2,0,1:T(8,128)} %get-tuple-element.504, s32[]{:T(128)S(6)} %select_n.170, s32[192,128]{1,0:T(8,128)S(1)} %copy.159), kind=kOutput, calls=%fused_computation.27.clone.1 | convolution fusion | flops 758120448 | bytes 4423684 | tf_op jit(solution)/shard_map/while/body/eval_jaxpr/ctk,tks->cts/dot_general | solution.py:107
  306.5 91.0 %all-reduce.7.cloned.1.call-done = f32[20,16384]{1,0:T(8,128)} async-done(((f32[20,16384]{1,0:T(8,128)}), f32[20,16384]{1,0:T(8,128)}) %all-reduce.7.cloned.1.call-update) | async-done | bytes 1310736 | tf_op jit(solution)/shard_map/psum | solution.py:189
  397.5 5.2 fusion.141
  418.9 40.0 %all-gather.2.cloned.1.call-done = f32[5,131072]{1,0:T(8,128)} async-done(((f32[5,16384]{1,0:T(8,128)}), f32[5,131072]{1,0:T(8,128)}) %all-gather.2.cloned.1.call-update) | async-done | bytes 2621456 | tf_op jit(solution)/shard_map/all_gather | solution.py:191
  462.8 55.2 %while.31 = (s32[]{:T(128)}, f32[5,512,128]{2,1,0:T(8,128)}, s32[512,128]{0,1:T(8,128)S(1)}, f32[5,1024,128]{2,1,0:T(8,128)S(1)}, s32[]{:T(128)}, /*index=5*/s32[]{:T(128)}, s32[]{:T(128)}, s32[]{:T(128)}) while((s32[]{:T(128)}, f32[5,512,128]{2,1,0:T(8,128)}, s32[512,128]{0,1:T(8,128)S(1)}, f32[5,1024,128]{2,1,0:T(8,128)S(1)}, s32[]{:T(128)}, ...), condition=%wide.region_5.6_spmd, body=%wide.region_4.5_spmd.sunk | while | flops 567436224 | bytes 3605391 | solution.py:135
  464.2 4.8 fusion.203
  471.1 4.8 fusion.203
  478.0 4.8 fusion.203
  484.9 4.8 fusion.203
  491.8 4.8 fusion.203
  498.7 4.8 fusion.203
  505.6 4.8 fusion.203
  512.5 4.8 fusion.203
  531.4 25.9 %psum.15 = f32[14,512]{1,0:T(8,128)S(1)} all-reduce(f32[14,512]{1,0:T(8,128)S(1)} %slice_add_fusion.5), channel_id=1, replica_groups=mesh['tm'=4,'sky'=8] {'sky'}, use_global_device_ids=true, to_apply=%region_62.63 | all-reduce | flops 7168 | bytes 57344 | tf_op jit(solution)/shard_map/psum | solution.py:205
  (196 shorter events, 140.7 us)
Async XLA Ops:
  26.2 9.7 %copy-start.7 = (s32[512,128]{1,0:T(8,128)S(1)}, s32[512,128]{1,0:T(8,128)}, u32[]{:S(2)}) copy-start(s32[512,128]{1,0:T(8,128)} %param.16) | copy-start | bytes 786436
  29.9 15.6 %collective-permute-start = (f32[6,192,128]{2,1,0:T(8,128)}, f32[6,192,128]{2,1,0:T(8,128)}, u32[]{:S(2)}, u32[]{:S(2)}) collective-permute-start(f32[6,192,128]{2,1,0:T(8,128)} %get-tuple-element.411), channel_id=1, source_target_pairs={{0,1},{1,0},{2,3},{3,2},{4,5},{5,4},{6,7},{7,6},{8,9},{9,8},{10,11... | collective-permute-start | bytes 1769480 | tf_op jit(solution)/shard_map/ppermute | solution.py:31
  30.4 41.9 %collective-permute-start.1 = (f32[6,192,128]{2,1,0:T(8,128)}, f32[6,192,128]{2,1,0:T(8,128)}, u32[]{:S(2)}, u32[]{:S(2)}) collective-permute-start(f32[6,192,128]{2,1,0:T(8,128)} %get-tuple-element.410), channel_id=1, source_target_pairs={{0,2},{1,3},{2,0},{3,1},{4,6},{5,7},{6,4},{7,5},{8,10},{9,11},{10,... | collective-permute-start | bytes 1769480 | tf_op jit(solution)/shard_map/ppermute | solution.py:31
  33.0 51.7 %collective-permute-start.2 = (f32[6,192,128]{2,1,0:T(8,128)}, f32[6,192,128]{2,1,0:T(8,128)}, u32[]{:S(2)}, u32[]{:S(2)}) collective-permute-start(f32[6,192,128]{2,1,0:T(8,128)} %get-tuple-element.409), channel_id=1, source_target_pairs={{0,3},{1,2},{2,1},{3,0},{4,7},{5,6},{6,5},{7,4},{8,11},{9,10},{10,... | collective-permute-start | bytes 1769480 | tf_op jit(solution)/shard_map/ppermute | solution.py:31
  33.1 53.5 %collective-permute-start.3 = (f32[6,192,128]{2,1,0:T(8,128)}, f32[6,192,128]{2,1,0:T(8,128)}, u32[]{:S(2)}, u32[]{:S(2)}) collective-permute-start(f32[6,192,128]{2,1,0:T(8,128)} %get-tuple-element.408), channel_id=1, source_target_pairs={{0,4},{1,5},{2,6},{3,7},{4,0},{5,1},{6,2},{7,3},{8,12},{9,13},{10,... | collective-permute-start | bytes 1769480 | tf_op jit(solution)/shard_map/ppermute | solution.py:31
  35.8 52.6 %collective-permute-start.4 = (f32[6,192,128]{2,1,0:T(8,128)S(1)}, f32[6,192,128]{2,1,0:T(8,128)}, u32[]{:S(2)}, u32[]{:S(2)}) collective-permute-start(f32[6,192,128]{2,1,0:T(8,128)S(1)} %get-tuple-element.407), channel_id=1, source_target_pairs={{0,5},{1,4},{2,7},{3,6},{4,1},{5,0},{6,3},{7,2},{8,13},{9,12},{10,... | collective-permute-start | bytes 1769480 | tf_op jit(solution)/shard_map/ppermute | solution.py:31
  38.4 150.9 %all-to-all-start = ((s32[1,1536,128]{2,0,1:T(1,128)}), s32[1,1536,128]{2,0,1:T(1,128)}, u32[]{:S(2)}, u32[]{:S(2)}) async-start(s32[1,1536,128]{2,0,1:T(1,128)} %bitcast.7), calls=%async_computation | async-start | bytes 1572864 | tf_op jit(solution)/shard_map/all_to_all | solution.py:183
  43.3 354.2 %all-reduce.7.cloned.1.call-start = ((), (), s32[]{:S(2)}) async-start(), calls=%async_computation.1 | async-start | bytes 3145728 | tf_op jit(solution)/shard_map/psum | solution.py:189
  45.5 67.7 %collective-permute-start.5 = (f32[6,192,128]{2,1,0:T(8,128)S(1)}, f32[6,192,128]{2,1,0:T(8,128)S(1)}, u32[]{:S(2)}, u32[]{:S(2)}) collective-permute-start(f32[6,192,128]{2,1,0:T(8,128)S(1)} %get-tuple-element.406), channel_id=1, source_target_pairs={{0,6},{1,7},{2,4},{3,5},{4,2},{5,3},{6,0},{7,1},{8,14},{9,15},{10,... | collective-permute-start | bytes 1769480 | tf_op jit(solution)/shard_map/ppermute | solution.py:31
  72.4 52.5 %collective-permute-start.6 = (f32[6,192,128]{2,1,0:T(8,128)S(1)}, f32[6,192,128]{2,1,0:T(8,128)S(1)}, u32[]{:S(2)}, u32[]{:S(2)}) collective-permute-start(f32[6,192,128]{2,1,0:T(8,128)S(1)} %get-tuple-element.405), channel_id=1, source_target_pairs={{0,7},{1,6},{2,5},{3,4},{4,3},{5,2},{6,1},{7,0},{8,15},{9,14},{10,... | collective-permute-start | bytes 1769480 | tf_op jit(solution)/shard_map/ppermute | solution.py:31
  131.2 5.3 slice-start
  131.2 5.3 slice-start.1
  306.4 105.7 %copy-start.9 = (s32[512]{0:T(512)S(1)}, s32[512]{0:T(512)}, u32[]{:S(2)}) copy-start(s32[512]{0:T(512)} %param.18) | copy-start | bytes 6148
  306.4 105.7 %copy-start.1 = (f32[512,128]{1,0:T(8,128)S(1)}, f32[512,128]{1,0:T(8,128)}, u32[]{:S(2)}) copy-start(f32[512,128]{1,0:T(8,128)} %param.13) | copy-start | bytes 786436
  306.4 152.5 %all-gather.2.cloned.1.call-start = ((), (), s32[]{:S(2)}) async-start(), calls=%async_computation.2 | async-start | bytes 4718592 | tf_op jit(solution)/shard_map/all_gather | solution.py:191
  518.0 3.7 copy-start
  518.0 3.7 copy-start.2
  518.0 3.8 copy-start.3
  518.0 3.9 copy-start.4
  518.0 3.9 copy-start.5
  518.0 4.0 copy-start.6
  526.6 4.7 collective-permute-start.7
  557.5 13.0 %copy-start.8 = (f32[4,512]{1,0:T(4,128)}, f32[4,512]{1,0:T(4,128)S(1)}, u32[]{:S(2)}) copy-start(f32[4,512]{1,0:T(4,128)S(1)} %pad_maximum_fusion.1) | copy-start | bytes 24580
  558.2 5.7 collective-permute-start.8
Sparse Core Ops, SparseCore 0:
  306.5 90.9 all-reduce.6
  412.0 46.8 all-gather.1
